TPU v7x, 32 devices: a whole 2x2x4 slice. The times are simulated.
32 devices in a mesh: rows: 8 (over z, x), cols: 4 (over y, core).
Axes of the slice: x: 2, y: 2, z: 4, core: 2. Of those that a mesh axis runs over, the one named last changes fastest.
Arguments:
- matrix: float32 [512, 32, 2, 128], P('rows', 'cols'), may hold values from -54 to 54
- plan: int32 [2, 4, 256], replicated, may hold values from 0 to 255, as said below
Outputs:
- rotated: float32 [512, 32, 2, 128], P('rows', 'cols')
Inputs may be any that keep to these rules, and one draw needn't show every extreme that they name: Each plan[s, r] pairs the 256 columns: partner of partner of i is i, and no column is its own partner.
All inputs are finite; a program needn't handle non-finite values.
Results may differ from a plain program's by a relative error of at most 0.0003.
Values sent between devices are 32-bit elements; how exact they have to be, the bound alone decides.
A program may use at most 128 MiB of HBM per device.

v0:
```python
import jax
import jax.numpy as jnp
from jax import lax
from jax.sharding import PartitionSpec as P

STEPS = 2


def passed_along(block, axis, distance):
    devices = range(lax.axis_size(axis))
    route = [((i - distance) % len(devices), i) for i in devices]
    return lax.ppermute(block, axis, route)


def diagonalize(grams, table):
    width = grams.shape[1]
    indices = jnp.arange(width, dtype=jnp.int32)
    rotation = jnp.broadcast_to(jnp.eye(width, dtype=jnp.float32), grams.shape)
    unit_matrix = jnp.eye(width, dtype=jnp.float32)
    for round_index in range(table.shape[0]):
        partner = table[round_index]
        onehot = (partner[:, None] == indices[None, :]).astype(jnp.float32)
        diagonal_now = jnp.diagonal(grams, axis1=1, axis2=2)
        partner_diag = jnp.einsum(
            "pj,ij->pi", diagonal_now, onehot, precision=lax.Precision.HIGHEST
        )
        partner_gram = jnp.sum(grams * onehot[None], axis=2)
        orient = jnp.where(indices < partner, 1.0, -1.0).astype(jnp.float32)
        spread = orient[None, :] * (partner_diag - diagonal_now)
        sign_part = jnp.where(spread >= 0.0, 1.0, -1.0).astype(jnp.float32)
        tangent = (
            sign_part
            * 2.0
            * partner_gram
            / (jnp.abs(spread) + jnp.sqrt(spread * spread + 4.0 * partner_gram * partner_gram))
        )
        cosine = 1.0 / jnp.sqrt(1.0 + tangent * tangent)
        sine_part = tangent * cosine
        off_part = jnp.swapaxes(onehot[None] * (-orient[None, :] * sine_part)[:, :, None], 1, 2)
        rot_now = cosine[:, :, None] * unit_matrix[None] + off_part
        product = jnp.einsum("pij,pjk->pik", grams, rot_now, precision=lax.Precision.HIGHEST)
        grams = jnp.einsum("pji,pjk->pik", rot_now, product, precision=lax.Precision.HIGHEST)
        rotation = jnp.einsum("pij,pjk->pik", rotation, rot_now, precision=lax.Precision.HIGHEST)
    return (grams, rotation)


def full_grams(columns):
    local_sum = jnp.einsum("mpi,mpj->pij", columns, columns, precision=lax.Precision.HIGHEST)
    return lax.psum(local_sum, "rows")


def body(matrix, plan):
    rows_here, pair_here, halves, width = matrix.shape
    columns = matrix.reshape(rows_here, pair_here, halves * width)
    grams = full_grams(columns)
    for step_index in range(STEPS):
        grams, rotation = diagonalize(grams, plan[step_index])
        columns = jnp.einsum("mpi,pij->mpj", columns, rotation, precision=lax.Precision.HIGHEST)
        quarter = columns.reshape(rows_here, pair_here, halves, width)
        tops = quarter[:, :, 0, :]
        bottoms = quarter[:, :, 1, :]
        bottoms, low_grams = passed_along((bottoms, grams[:, width:, width:]), "cols", 1)
        columns = jnp.stack([tops, bottoms], axis=2).reshape(rows_here, pair_here, halves * width)
        if step_index + 1 < STEPS:
            cross_local = jnp.einsum("mpi,mpj->pij", tops, bottoms, precision=lax.Precision.HIGHEST)
            cross = lax.psum(cross_local, "rows")
            upper_rows = jnp.concatenate([grams[:, :width, :width], cross], axis=2)
            lower_rows = jnp.concatenate([jnp.swapaxes(cross, 1, 2), low_grams], axis=2)
            grams = jnp.concatenate([upper_rows, lower_rows], axis=1)
    return columns.reshape(matrix.shape)


def solution(mesh):
    in_specs = (P("rows", "cols", None, None), P())
    out_specs = P("rows", "cols", None, None)
    return jax.shard_map(body, mesh=mesh, in_specs=in_specs, out_specs=out_specs, check_vma=False)
```

profile of v0, /device:TPU:0, one launch (start us, length us, event | category | flops | bytes accessed | tf_op | source)
XLA Modules:
  0.0 463.2 jit_solution(2592383849989567668)
XLA Ops:
  8.0 3.2 fusion.123
  24.4 92.0 %all-reduce.3.cloned.1.call-done = f32[8,256,256]{2,1,0:T(8,128)} async-done(((f32[8,256,256]{2,1,0:T(8,128)}), f32[8,256,256]{2,1,0:T(8,128)}) %all-reduce.3.cloned.1.call-update) | async-done | bytes 2097168 | tf_op jit(solution)/shard_map/psum | solution.py:49
  116.4 17.5 %copy.30 = f32[8,256,256]{0,2,1:T(8,128)} copy(f32[8,256,256]{2,1,0:T(8,128)} %all-reduce.3.cloned.1.call-done) | data formatting | bytes 4194304 | tf_op jit(solution)/shard_map/psum | solution.py:49
  138.7 3.5 fusion.22
  142.2 4.1 fusion.24
  146.3 3.3 multiply_reduce_fusion.6
  149.6 16.5 %copy.32 = f32[8,256,256]{0,2,1:T(8,128)} copy(f32[8,256,256]{1,2,0:T(8,128)S(1)} %get-tuple-element.56) | data formatting | bytes 4194304 | tf_op jit(solution)/shard_map/pji,pjk->pik/dot_general | solution.py:42
  170.1 5.1 %fusion.21 = f32[8,256,256]{1,2,0:T(8,128)S(1)} fusion(f32[8,256,256]{1,2,0:T(8,128)S(1)} %get-tuple-element.56, f32[8,256]{1,0:T(8,128)S(1)} %get-tuple-element.34, f32[256,256]{1,0:T(8,128)} %fusion.135, f32[8,256]{1,0:T(8,128)S(1)} %get-tuple-element.33, f32[256,256]{1,0:T(8,128)S(1)} %get-tuple-element.67), kind=kOutput, calls=%fused_computation.42 | convolution fusion | flops 1612185600 | bytes 4734976 | tf_op jit(solution)/shard_map/pij,pjk->pik/dot_general | solution.py:41
  175.2 3.3 multiply_reduce_fusion.5
  178.6 16.6 %copy.34 = f32[8,256,256]{0,2,1:T(8,128)} copy(f32[8,256,256]{1,2,0:T(8,128)S(1)} %get-tuple-element.58) | data formatting | bytes 4194304 | tf_op jit(solution)/shard_map/pji,pjk->pik/dot_general | solution.py:42
  199.3 5.1 %fusion.18 = f32[8,256,256]{1,2,0:T(8,128)S(1)} fusion(f32[8,256,256]{1,2,0:T(8,128)S(1)} %get-tuple-element.58, f32[8,256]{1,0:T(8,128)S(1)} %get-tuple-element.32, f32[256,256]{1,0:T(8,128)} %fusion.136, f32[8,256]{1,0:T(8,128)S(1)} %get-tuple-element.31, f32[256,256]{1,0:T(8,128)S(1)} %get-tuple-element.67), kind=kOutput, calls=%fused_computation.37 | convolution fusion | flops 1612185600 | bytes 4734976 | tf_op jit(solution)/shard_map/pij,pjk->pik/dot_general | solution.py:41
  204.4 3.3 multiply_reduce_fusion.4
  207.8 16.4 %copy.36 = f32[8,256,256]{0,2,1:T(8,128)} copy(f32[8,256,256]{1,2,0:T(8,128)S(1)} %get-tuple-element.60) | data formatting | bytes 4194304 | tf_op jit(solution)/shard_map/pji,pjk->pik/dot_general | solution.py:42
  228.2 5.1 %fusion.15 = f32[8,256,256]{1,2,0:T(8,128)S(1)} fusion(f32[8,256,256]{1,2,0:T(8,128)S(1)} %get-tuple-element.60, f32[8,256]{1,0:T(8,128)S(1)} %get-tuple-element.30, f32[256,256]{1,0:T(8,128)} %fusion.137, f32[8,256]{1,0:T(8,128)S(1)} %get-tuple-element.29, f32[256,256]{1,0:T(8,128)S(1)} %get-tuple-element.67), kind=kOutput, calls=%fused_computation.32 | convolution fusion | flops 1612185600 | bytes 4734976 | tf_op jit(solution)/shard_map/pij,pjk->pik/dot_general | solution.py:41
  238.5 2.7 fusion.16
  252.7 3.1 collective-permute-done
  259.6 70.2 %all-reduce.5.cloned.1.call-done = f32[8,128,128]{1,2,0:T(8,128)} async-done(((f32[8,128,128]{1,2,0:T(8,128)}), f32[8,128,128]{1,2,0:T(8,128)}) %all-reduce.5.cloned.1.call-update) | async-done | bytes 524304 | tf_op jit(solution)/shard_map/psum | solution.py:66
  333.6 16.7 %copy.43 = f32[8,256,256]{0,2,1:T(8,128)} copy(f32[8,256,256]{1,2,0:T(8,128)S(1)} %get-tuple-element.5) | data formatting | bytes 4194304 | tf_op jit(solution)/shard_map/concatenate | solution.py:69
  353.1 3.5 fusion.12
  356.6 4.1 fusion.11
  360.7 2.7 multiply_reduce_fusion.2
  363.5 16.4 %copy.45 = f32[8,256,256]{0,2,1:T(8,128)} copy(f32[8,256,256]{1,2,0:T(8,128)S(1)} %get-tuple-element.62) | data formatting | bytes 4194304 | tf_op jit(solution)/shard_map/pji,pjk->pik/dot_general | solution.py:42
  382.6 4.1 fusion.8
  386.8 3.8 fusion.9
  390.5 2.7 multiply_reduce_fusion.1
  393.3 16.5 %copy.47 = f32[8,256,256]{0,2,1:T(8,128)} copy(f32[8,256,256]{1,2,0:T(8,128)S(1)} %get-tuple-element.64) | data formatting | bytes 4194304 | tf_op jit(solution)/shard_map/pji,pjk->pik/dot_general | solution.py:42
  412.5 4.1 fusion.5
  416.6 3.8 fusion.6
  420.4 2.7 multiply_reduce_fusion
  423.1 16.5 %copy.49 = f32[8,256,256]{0,2,1:T(8,128)} copy(f32[8,256,256]{1,2,0:T(8,128)S(1)} %get-tuple-element.66) | data formatting | bytes 4194304 | tf_op jit(solution)/shard_map/pji,pjk->pik/dot_general | solution.py:42
  442.3 4.1 fusion
  449.0 5.8 %collective-permute-done.2 = f32[64,8,128]{2,1,0:T(8,128)S(1)} collective-permute-done((f32[64,8,128]{2,1,0:T(8,128)S(1)}, f32[64,8,128]{2,1,0:T(8,128)S(1)}, u32[]{:S(2)}, u32[]{:S(2)}) %collective-permute-start.2) | collective-permute-done | bytes 262176 | tf_op jit(solution)/shard_map/ppermute | solution.py:12
  (172 shorter events, 70.0 us)
Async XLA Ops:
  6.5 109.9 %all-reduce.3.cloned.1.call-start = ((), (), s32[]{:S(2)}) async-start(), calls=%async_computation | async-start | bytes 4194304 | tf_op jit(solution)/shard_map/psum | solution.py:49
  11.2 318.5 %all-reduce.5.cloned.1.call-start = ((), (), s32[]{:S(2)}) async-start(), calls=%async_computation.1 | async-start | bytes 1048576 | tf_op jit(solution)/shard_map/psum | solution.py:66
  11.5 12.9 %copy-start.31 = (s32[1,1,256]{2,1,0:T(1,128)}, s32[1,1,256]{2,1,0:T(1,128)S(1)}, u32[]{:S(2)}) copy-start(s32[1,1,256]{2,1,0:T(1,128)S(1)} %get-tuple-element.22) | copy-start | bytes 3076
  11.5 12.9 %copy-start.33 = (s32[1,1,256]{2,1,0:T(1,128)}, s32[1,1,256]{2,1,0:T(1,128)S(1)}, u32[]{:S(2)}) copy-start(s32[1,1,256]{2,1,0:T(1,128)S(1)} %get-tuple-element.16) | copy-start | bytes 3076
  11.5 12.9 %copy-start.35 = (s32[1,1,256]{2,1,0:T(1,128)}, s32[1,1,256]{2,1,0:T(1,128)S(1)}, u32[]{:S(2)}) copy-start(s32[1,1,256]{2,1,0:T(1,128)S(1)} %get-tuple-element.21) | copy-start | bytes 3076
  11.5 12.9 %copy-start.37 = (s32[1,1,256]{2,1,0:T(1,128)}, s32[1,1,256]{2,1,0:T(1,128)S(1)}, u32[]{:S(2)}) copy-start(s32[1,1,256]{2,1,0:T(1,128)S(1)} %get-tuple-element.20) | copy-start | bytes 3076
  11.5 12.9 %copy-start.38 = (s32[1,1,256]{2,1,0:T(1,128)}, s32[1,1,256]{2,1,0:T(1,128)S(1)}, u32[]{:S(2)}) copy-start(s32[1,1,256]{2,1,0:T(1,128)S(1)} %get-tuple-element.19) | copy-start | bytes 3076
  11.5 12.9 %copy-start.39 = (s32[1,1,256]{2,1,0:T(1,128)}, s32[1,1,256]{2,1,0:T(1,128)S(1)}, u32[]{:S(2)}) copy-start(s32[1,1,256]{2,1,0:T(1,128)S(1)} %get-tuple-element.18) | copy-start | bytes 3076
  11.6 12.9 %copy-start.40 = (s32[1,1,256]{2,1,0:T(1,128)}, s32[1,1,256]{2,1,0:T(1,128)S(1)}, u32[]{:S(2)}) copy-start(s32[1,1,256]{2,1,0:T(1,128)S(1)} %get-tuple-element.17) | copy-start | bytes 3076
  116.4 19.9 %copy-start = (f32[8,256,256]{2,1,0:T(8,128)S(1)}, f32[8,256,256]{2,1,0:T(8,128)}, u32[]{:S(2)}) copy-start(f32[8,256,256]{2,1,0:T(8,128)} %all-reduce.3.cloned.1.call-done) | copy-start | bytes 6291460
  199.2 5.2 %copy-start.27 = (f32[8,256]{1,0:T(8,128)}, f32[8,256]{1,0:T(8,128)S(1)}, u32[]{:S(2)}) copy-start(f32[8,256]{1,0:T(8,128)S(1)} %get-tuple-element.31) | copy-start | bytes 24580
  199.2 5.2 %copy-start.29 = (f32[8,256]{1,0:T(8,128)}, f32[8,256]{1,0:T(8,128)S(1)}, u32[]{:S(2)}) copy-start(f32[8,256]{1,0:T(8,128)S(1)} %get-tuple-element.32) | copy-start | bytes 24580
  199.2 5.2 %copy-start.6 = (f32[256,256]{1,0:T(8,128)S(1)}, f32[256,256]{1,0:T(8,128)}, u32[]{:S(2)}) copy-start(f32[256,256]{1,0:T(8,128)} %fusion.136) | copy-start | bytes 786436
  199.3 5.2 %copy-start.20 = (f32[256,256]{0,1:T(8,128)S(1)}, f32[256,256]{0,1:T(8,128)}, u32[]{:S(2)}) copy-start(f32[256,256]{0,1:T(8,128)} %fusion.129) | copy-start | bytes 786436
  250.0 5.8 %collective-permute-start = (f32[64,8,128]{2,0,1:T(8,128)S(1)}, f32[64,8,128]{2,0,1:T(8,128)S(1)}, u32[]{:S(2)}, u32[]{:S(2)}) collective-permute-start(f32[64,8,128]{2,0,1:T(8,128)S(1)} %bitcast.109), channel_id=1, source_target_pairs={{3,0},{0,1},{1,2},{2,3},{7,4},{4,5},{5,6},{6,7},{11,8},{8,9},{9,10... | collective-permute-start | bytes 786440 | tf_op jit(solution)/shard_map/ppermute | solution.py:12
  251.1 79.9 %collective-permute-start.1 = (f32[8,128,128]{1,2,0:T(8,128)}, f32[8,128,128]{1,2,0:T(8,128)S(1)}, u32[]{:S(2)}, u32[]{:S(2)}) collective-permute-start(f32[8,128,128]{1,2,0:T(8,128)} %get-tuple-element.8), channel_id=1, source_target_pairs={{3,0},{0,1},{1,2},{2,3},{7,4},{4,5},{5,6},{6,7},{11,8},{8,9},{9,10... | collective-permute-start | bytes 1572872 | tf_op jit(solution)/shard_map/ppermute | solution.py:12
  333.6 19.2 %copy-start.36 = (s32[1,1,256]{2,1,0:T(1,128)S(1)}, s32[1,1,256]{2,1,0:T(1,128)}, u32[]{:S(2)}) copy-start(s32[1,1,256]{2,1,0:T(1,128)} %copy-done.35) | copy-start | bytes 3076
  333.6 19.2 %copy-start.46 = (f32[256]{0:T(256)S(1)}, f32[256]{0:T(256)}, u32[]{:S(2)}) copy-start(f32[256]{0:T(256)} %get-tuple-element.43) | copy-start | bytes 3076
  333.6 19.2 %copy-start.47 = (f32[256]{0:T(256)S(1)}, f32[256]{0:T(256)}, u32[]{:S(2)}) copy-start(f32[256]{0:T(256)} %get-tuple-element.44) | copy-start | bytes 3076
  333.6 19.5 %copy-start.10 = (f32[256,256]{1,0:T(8,128)S(1)}, f32[256,256]{1,0:T(8,128)}, u32[]{:S(2)}) copy-start(f32[256,256]{1,0:T(8,128)} %fusion.138) | copy-start | bytes 786436
  350.3 6.2 %copy-start.11 = (f32[8,128,128]{1,2,0:T(8,128)S(1)}, f32[8,128,128]{1,2,0:T(8,128)}, u32[]{:S(2)}) copy-start(f32[8,128,128]{1,2,0:T(8,128)} %all-reduce.5.cloned.1.call-done) | copy-start | bytes 1572868
  350.3 6.2 %copy-start.13 = (f32[8,128,128]{1,2,0:T(8,128)S(1)}, f32[8,128,128]{1,2,0:T(8,128)}, u32[]{:S(2)}) copy-start(f32[8,128,128]{1,2,0:T(8,128)} %copy-done.12) | copy-start | bytes 1572868
  350.3 6.2 %copy-start.14 = (f32[8,128,128]{1,2,0:T(8,128)S(1)}, f32[8,128,128]{1,2,0:T(8,128)}, u32[]{:S(2)}) copy-start(f32[8,128,128]{1,2,0:T(8,128)} %get-tuple-element.7) | copy-start | bytes 1572868
  350.3 6.2 %copy-start.24 = (f32[8,128,128]{1,2,0:T(8,128)S(1)}, f32[8,128,128]{1,2,0:T(8,128)}, u32[]{:S(2)}) copy-start(f32[8,128,128]{1,2,0:T(8,128)} %copy-done.23) | copy-start | bytes 1572868
  363.5 18.9 %copy-start.34 = (s32[1,1,256]{2,1,0:T(1,128)S(1)}, s32[1,1,256]{2,1,0:T(1,128)}, u32[]{:S(2)}) copy-start(s32[1,1,256]{2,1,0:T(1,128)} %copy-done.33) | copy-start | bytes 3076
  363.5 18.9 %copy-start.44 = (f32[256]{0:T(256)S(1)}, f32[256]{0:T(256)}, u32[]{:S(2)}) copy-start(f32[256]{0:T(256)} %get-tuple-element.41) | copy-start | bytes 3076
  363.5 18.8 %copy-start.45 = (f32[256]{0:T(256)S(1)}, f32[256]{0:T(256)}, u32[]{:S(2)}) copy-start(f32[256]{0:T(256)} %get-tuple-element.42) | copy-start | bytes 3076
  393.3 18.9 %copy-start.32 = (s32[1,1,256]{2,1,0:T(1,128)S(1)}, s32[1,1,256]{2,1,0:T(1,128)}, u32[]{:S(2)}) copy-start(s32[1,1,256]{2,1,0:T(1,128)} %copy-done.31) | copy-start | bytes 3076
  393.3 18.9 %copy-start.42 = (f32[256]{0:T(256)S(1)}, f32[256]{0:T(256)}, u32[]{:S(2)}) copy-start(f32[256]{0:T(256)} %get-tuple-element.39) | copy-start | bytes 3076
  393.3 18.9 %copy-start.43 = (f32[256]{0:T(256)S(1)}, f32[256]{0:T(256)}, u32[]{:S(2)}) copy-start(f32[256]{0:T(256)} %get-tuple-element.40) | copy-start | bytes 3076
  423.1 19.2 %copy-start.19 = (f32[256,256]{1,0:T(8,128)S(1)}, f32[256,256]{1,0:T(8,128)}, u32[]{:S(2)}) copy-start(f32[256,256]{1,0:T(8,128)} %fusion.141) | copy-start | bytes 786436
  449.0 5.8 %collective-permute-start.2 = (f32[64,8,128]{2,1,0:T(8,128)S(1)}, f32[64,8,128]{2,1,0:T(8,128)S(1)}, u32[]{:S(2)}, u32[]{:S(2)}) collective-permute-start(f32[64,8,128]{2,1,0:T(8,128)S(1)} %bitcast.108), channel_id=1, source_target_pairs={{3,0},{0,1},{1,2},{2,3},{7,4},{4,5},{5,6},{6,7},{11,8},{8,9},{9,10... | collective-permute-start | bytes 786440 | tf_op jit(solution)/shard_map/ppermute | solution.py:12
  (21 other events, 73.5 us)
Sparse Core Ops, SparseCore 0:
  11.4 105.0 all-reduce.2
  257.8 71.9 all-reduce.4
where the time goes:
time: 467 us; the launch traced here: 463 us
  waiting for transfers between devices  171 us (37%)
  local copies, waits for them, and re-layouts  165 us (35%)
  matrix products  92.9 us (20%)
  other arithmetic  18 us (4%)
  between operations  14.6 us (3%)
    dot_general x6, local copies, waits for them, and re-layouts, diagonalize(): jnp.einsum('pji,pjk->pik', rot_now, product, precision=lax.Precision.HIGH...  98.9 us
    psum x1, waiting for transfers between devices, full_grams(): return lax.psum(local_sum, 'rows')  92 us
    psum x1, waiting for transfers between devices, body(): cross = lax.psum(cross_local, 'rows')  70.2 us
    dot_general x7, matrix products, diagonalize(): jnp.einsum('pij,pjk->pik', grams, rot_now, precision=lax.Precision.HIGHEST)  31.7 us
    dot_general x8, matrix products, diagonalize(): jnp.einsum('pij,pjk->pik', rotation, rot_now, precision=lax.Precision.HIG...  26.3 us
    gather x16, local copies, waits for them, and re-layouts, diagonalize(): diagonal_now = jnp.diagonal(grams, axis1=1, axis2=2)  21 us
    dot_general x7, matrix products, diagonalize(): jnp.einsum('pji,pjk->pik', rot_now, product, precision=lax.Precision.HIGH...  20.8 us
    psum x1, local copies, waits for them, and re-layouts, full_grams(): return lax.psum(local_sum, 'rows')  17.5 us
  transfers between devices with their start and end apart: 5, of which 4 were waited for; matrix products, arithmetic and copies ran while one was open for 4% of the time, Pallas kernels for 0%

commit v1 on v0

--- a/solution.py
+++ b/solution.py
@@ -46,7 +46,7 @@
 
 def full_grams(columns):
     local_sum = jnp.einsum("mpi,mpj->pij", columns, columns, precision=lax.Precision.HIGHEST)
-    return lax.psum(local_sum, "rows")
+    return jnp.sum(jax.lax.all_gather(local_sum, axis_name="rows"), axis=0)
 
 
 def body(matrix, plan):

time: 467 us -> 601 us (1.29)
  waiting for transfers between devices: 171 us -> 295 us
  other arithmetic: 18 us -> 25.2 us
    all_gather x0 -> x1, waiting for transfers between devices: none -> 217 us  [full_grams(): return jnp.sum(jax.lax.all_gather(local_sum, axis_name='rows'), axis=0)]
    psum x1 -> x0, waiting for transfers between devices: 92 us -> none  [full_grams(): return lax.psum(local_sum, 'rows')]
    psum x1 -> x0, local copies, waits for them, and re-layouts: 17.5 us -> none  [full_grams(): return lax.psum(local_sum, 'rows')]
    reduce_sum x0 -> x1, local copies, waits for them, and re-layouts: none -> 16.8 us  [full_grams(): return jnp.sum(jax.lax.all_gather(local_sum, axis_name='rows'), axis=0)]
    reduce_sum x0 -> x1, other arithmetic: none -> 7.24 us  [full_grams(): return jnp.sum(jax.lax.all_gather(local_sum, axis_name='rows'), axis=0)]
  transfers between devices with their start and end apart: 5 -> 5, of which waited for: 4 -> 4; matrix products, arithmetic and copies ran while one was open for 4% -> 3% of each run, Pallas kernels for 0% -> 0%
where the time goes in v1:
time: 601 us; the launch traced here: 596 us
  waiting for transfers between devices  295 us (49%)
  local copies, waits for them, and re-layouts  165 us (27%)
  matrix products  94 us (16%)
  other arithmetic  25.2 us (4%)
  between operations  14.7 us (2%)
    all_gather x1, waiting for transfers between devices, full_grams(): return jnp.sum(jax.lax.all_gather(local_sum, axis_name='rows'), axis=0)  217 us
    dot_general x6, local copies, waits for them, and re-layouts, diagonalize(): jnp.einsum('pji,pjk->pik', rot_now, product, precision=lax.Precision.HIGH...  99.8 us
    psum x1, waiting for transfers between devices, body(): cross = lax.psum(cross_local, 'rows')  69.1 us
    dot_general x7, matrix products, diagonalize(): jnp.einsum('pij,pjk->pik', grams, rot_now, precision=lax.Precision.HIGHEST)  32.7 us
    dot_general x8, matrix products, diagonalize(): jnp.einsum('pij,pjk->pik', rotation, rot_now, precision=lax.Precision.HIG...  26.3 us
    gather x16, local copies, waits for them, and re-layouts, diagonalize(): diagonal_now = jnp.diagonal(grams, axis1=1, axis2=2)  21.5 us
    dot_general x7, matrix products, diagonalize(): jnp.einsum('pji,pjk->pik', rot_now, product, precision=lax.Precision.HIGH...  20.8 us
    concatenate x1, local copies, waits for them, and re-layouts, body(): grams = jnp.concatenate([upper_rows, lower_rows], axis=1)  16.8 us
  transfers between devices with their start and end apart: 5, of which 4 were waited for; matrix products, arithmetic and copies ran while one was open for 3% of the time, Pallas kernels for 0%

profile of v1, /device:TPU:0, one launch (start us, length us, event | category | flops | bytes accessed | tf_op | source)
XLA Modules:
  0.0 596.1 jit_solution(5183554303513472831)
XLA Ops:
  8.0 3.2 fusion.123
  24.3 217.1 %all-gather.3.cloned.1.call-done = f32[64,256,256]{2,1,0:T(8,128)} async-done(((f32[8,256,256]{2,1,0:T(8,128)}), f32[64,256,256]{2,1,0:T(8,128)}) %all-gather.3.cloned.1.call-update) | async-done | bytes 16777232 | tf_op jit(solution)/shard_map/all_gather | solution.py:49
  241.4 7.2 %reduce_sum.81 = f32[8,256,256]{2,1,0:T(8,128)S(1)} reduce(f32[8,8,256,256]{3,2,1,0:T(8,128)} %bitcast.104, f32[]{:T(128)} %constant.28.clone.1), dimensions={0}, to_apply=%region_0.0 | reduce | flops 3670016 | bytes 18874372 | tf_op jit(solution)/shard_map/reduce_sum | solution.py:49
  248.6 16.8 %copy.55 = f32[8,256,256]{0,2,1:T(8,128)} copy(f32[8,256,256]{2,1,0:T(8,128)S(1)} %reduce_sum.81) | data formatting | bytes 4194304 | tf_op jit(solution)/shard_map/reduce_sum | solution.py:49
  270.8 5.0 fusion.24
  275.8 3.5 fusion.22
  279.3 3.3 multiply_reduce_fusion.6
  282.7 16.6 %copy.62 = f32[8,256,256]{0,2,1:T(8,128)} copy(f32[8,256,256]{1,2,0:T(8,128)S(1)} %get-tuple-element.56) | data formatting | bytes 4194304 | tf_op jit(solution)/shard_map/pji,pjk->pik/dot_general | solution.py:42
  303.3 5.1 fusion.21
  308.4 3.3 multiply_reduce_fusion.5
  311.8 16.8 %copy.66 = f32[8,256,256]{0,2,1:T(8,128)} copy(f32[8,256,256]{1,2,0:T(8,128)S(1)} %get-tuple-element.58) | data formatting | bytes 4194304 | tf_op jit(solution)/shard_map/pji,pjk->pik/dot_general | solution.py:42
  332.6 5.1 fusion.18
  337.7 3.3 multiply_reduce_fusion.4
  341.1 16.6 %copy.70 = f32[8,256,256]{0,2,1:T(8,128)} copy(f32[8,256,256]{1,2,0:T(8,128)S(1)} %get-tuple-element.60) | data formatting | bytes 4194304 | tf_op jit(solution)/shard_map/pji,pjk->pik/dot_general | solution.py:42
  361.6 5.1 fusion.15
  372.0 2.7 fusion.16
  386.2 3.1 collective-permute-done
  393.0 69.1 %all-reduce.2.cloned.1.call-done = f32[8,128,128]{1,2,0:T(8,128)} async-done(((f32[8,128,128]{1,2,0:T(8,128)}), f32[8,128,128]{1,2,0:T(8,128)}) %all-reduce.2.cloned.1.call-update) | async-done | bytes 524304 | tf_op jit(solution)/shard_map/psum | solution.py:66
  466.0 16.8 %copy.79 = f32[8,256,256]{0,2,1:T(8,128)} copy(f32[8,256,256]{1,2,0:T(8,128)S(1)} %get-tuple-element.5) | data formatting | bytes 4194304 | tf_op jit(solution)/shard_map/concatenate | solution.py:69
  485.6 3.5 fusion.12
  489.1 4.1 fusion.11
  493.2 2.7 multiply_reduce_fusion.2
  496.0 16.6 %copy.83 = f32[8,256,256]{0,2,1:T(8,128)} copy(f32[8,256,256]{1,2,0:T(8,128)S(1)} %get-tuple-element.62) | data formatting | bytes 4194304 | tf_op jit(solution)/shard_map/pji,pjk->pik/dot_general | solution.py:42
  515.3 4.1 fusion.8
  519.4 3.8 fusion.9
  526.0 16.6 %copy.87 = f32[8,256,256]{0,2,1:T(8,128)} copy(f32[8,256,256]{1,2,0:T(8,128)S(1)} %get-tuple-element.64) | data formatting | bytes 4194304 | tf_op jit(solution)/shard_map/pji,pjk->pik/dot_general | solution.py:42
  545.3 4.1 fusion.5
  549.4 3.8 fusion.6
  553.2 2.7 multiply_reduce_fusion
  555.9 16.7 %copy.91 = f32[8,256,256]{0,2,1:T(8,128)} copy(f32[8,256,256]{1,2,0:T(8,128)S(1)} %get-tuple-element.66) | data formatting | bytes 4194304 | tf_op jit(solution)/shard_map/pji,pjk->pik/dot_general | solution.py:42
  575.3 4.1 fusion
  582.0 5.8 collective-permute-done.2
  (171 shorter events, 73.1 us)
Async XLA Ops:
  6.5 234.9 %all-gather.3.cloned.1.call-start = ((), (), s32[]{:S(2)}) async-start(), calls=%async_computation.1 | async-start | bytes 18874368 | tf_op jit(solution)/shard_map/all_gather | solution.py:49
  11.2 450.9 %all-reduce.2.cloned.1.call-start = ((), (), s32[]{:S(2)}) async-start(), calls=%async_computation | async-start | bytes 1048576 | tf_op jit(solution)/shard_map/psum | solution.py:66
  11.3 12.9 %copy-start.30 = (s32[1,1,256]{2,1,0:T(1,128)}, s32[1,1,256]{2,1,0:T(1,128)S(1)}, u32[]{:S(2)}) copy-start(s32[1,1,256]{2,1,0:T(1,128)S(1)} %get-tuple-element.22) | copy-start | bytes 3076
  11.3 12.9 %copy-start.32 = (s32[1,1,256]{2,1,0:T(1,128)}, s32[1,1,256]{2,1,0:T(1,128)S(1)}, u32[]{:S(2)}) copy-start(s32[1,1,256]{2,1,0:T(1,128)S(1)} %get-tuple-element.16) | copy-start | bytes 3076
  11.4 12.9 %copy-start.34 = (s32[1,1,256]{2,1,0:T(1,128)}, s32[1,1,256]{2,1,0:T(1,128)S(1)}, u32[]{:S(2)}) copy-start(s32[1,1,256]{2,1,0:T(1,128)S(1)} %get-tuple-element.21) | copy-start | bytes 3076
  11.4 12.9 %copy-start.36 = (s32[1,1,256]{2,1,0:T(1,128)}, s32[1,1,256]{2,1,0:T(1,128)S(1)}, u32[]{:S(2)}) copy-start(s32[1,1,256]{2,1,0:T(1,128)S(1)} %get-tuple-element.20) | copy-start | bytes 3076
  11.4 12.9 %copy-start.37 = (s32[1,1,256]{2,1,0:T(1,128)}, s32[1,1,256]{2,1,0:T(1,128)S(1)}, u32[]{:S(2)}) copy-start(s32[1,1,256]{2,1,0:T(1,128)S(1)} %get-tuple-element.19) | copy-start | bytes 3076
  11.4 12.9 %copy-start.38 = (s32[1,1,256]{2,1,0:T(1,128)}, s32[1,1,256]{2,1,0:T(1,128)S(1)}, u32[]{:S(2)}) copy-start(s32[1,1,256]{2,1,0:T(1,128)S(1)} %get-tuple-element.18) | copy-start | bytes 3076
  11.4 12.9 %copy-start.39 = (s32[1,1,256]{2,1,0:T(1,128)}, s32[1,1,256]{2,1,0:T(1,128)S(1)}, u32[]{:S(2)}) copy-start(s32[1,1,256]{2,1,0:T(1,128)S(1)} %get-tuple-element.17) | copy-start | bytes 3076
  303.3 5.1 copy-start.24
  332.5 5.2 copy-start.26
  332.6 5.2 copy-start.28
  332.6 5.2 copy-start.4
  332.6 5.2 copy-start.19
  383.5 5.8 collective-permute-start
  384.6 78.8 %collective-permute-start.1 = (f32[8,128,128]{1,2,0:T(8,128)}, f32[8,128,128]{1,2,0:T(8,128)S(1)}, u32[]{:S(2)}, u32[]{:S(2)}) collective-permute-start(f32[8,128,128]{1,2,0:T(8,128)} %get-tuple-element.8), channel_id=1, source_target_pairs={{3,0},{0,1},{1,2},{2,3},{7,4},{4,5},{5,6},{6,7},{11,8},{8,9},{9,10... | collective-permute-start | bytes 1572872 | tf_op jit(solution)/shard_map/ppermute | solution.py:12
  466.0 19.3 %copy-start.35 = (s32[1,1,256]{2,1,0:T(1,128)S(1)}, s32[1,1,256]{2,1,0:T(1,128)}, u32[]{:S(2)}) copy-start(s32[1,1,256]{2,1,0:T(1,128)} %copy-done.34) | copy-start | bytes 3076
  466.0 19.3 %copy-start.45 = (f32[256]{0:T(256)S(1)}, f32[256]{0:T(256)}, u32[]{:S(2)}) copy-start(f32[256]{0:T(256)} %get-tuple-element.43) | copy-start | bytes 3076
  466.0 19.3 %copy-start.46 = (f32[256]{0:T(256)S(1)}, f32[256]{0:T(256)}, u32[]{:S(2)}) copy-start(f32[256]{0:T(256)} %get-tuple-element.44) | copy-start | bytes 3076
  466.0 19.6 %copy-start.9 = (f32[256,256]{1,0:T(8,128)S(1)}, f32[256,256]{1,0:T(8,128)}, u32[]{:S(2)}) copy-start(f32[256,256]{1,0:T(8,128)} %fusion.138) | copy-start | bytes 786436
  482.9 6.2 %copy-start.10 = (f32[8,128,128]{1,2,0:T(8,128)S(1)}, f32[8,128,128]{1,2,0:T(8,128)}, u32[]{:S(2)}) copy-start(f32[8,128,128]{1,2,0:T(8,128)} %all-reduce.2.cloned.1.call-done) | copy-start | bytes 1572868
  482.9 6.2 %copy-start.12 = (f32[8,128,128]{1,2,0:T(8,128)S(1)}, f32[8,128,128]{1,2,0:T(8,128)}, u32[]{:S(2)}) copy-start(f32[8,128,128]{1,2,0:T(8,128)} %copy-done.11) | copy-start | bytes 1572868
  482.9 6.2 %copy-start.13 = (f32[8,128,128]{1,2,0:T(8,128)S(1)}, f32[8,128,128]{1,2,0:T(8,128)}, u32[]{:S(2)}) copy-start(f32[8,128,128]{1,2,0:T(8,128)} %get-tuple-element.7) | copy-start | bytes 1572868
  482.9 6.2 %copy-start.23 = (f32[8,128,128]{1,2,0:T(8,128)S(1)}, f32[8,128,128]{1,2,0:T(8,128)}, u32[]{:S(2)}) copy-start(f32[8,128,128]{1,2,0:T(8,128)} %copy-done.22) | copy-start | bytes 1572868
  496.0 19.0 %copy-start.33 = (s32[1,1,256]{2,1,0:T(1,128)S(1)}, s32[1,1,256]{2,1,0:T(1,128)}, u32[]{:S(2)}) copy-start(s32[1,1,256]{2,1,0:T(1,128)} %copy-done.32) | copy-start | bytes 3076
  496.0 19.0 %copy-start.43 = (f32[256]{0:T(256)S(1)}, f32[256]{0:T(256)}, u32[]{:S(2)}) copy-start(f32[256]{0:T(256)} %get-tuple-element.41) | copy-start | bytes 3076
  496.0 19.0 %copy-start.44 = (f32[256]{0:T(256)S(1)}, f32[256]{0:T(256)}, u32[]{:S(2)}) copy-start(f32[256]{0:T(256)} %get-tuple-element.42) | copy-start | bytes 3076
  525.9 19.0 %copy-start.31 = (s32[1,1,256]{2,1,0:T(1,128)S(1)}, s32[1,1,256]{2,1,0:T(1,128)}, u32[]{:S(2)}) copy-start(s32[1,1,256]{2,1,0:T(1,128)} %copy-done.30) | copy-start | bytes 3076
  525.9 19.0 %copy-start.41 = (f32[256]{0:T(256)S(1)}, f32[256]{0:T(256)}, u32[]{:S(2)}) copy-start(f32[256]{0:T(256)} %get-tuple-element.39) | copy-start | bytes 3076
  526.0 19.0 %copy-start.42 = (f32[256]{0:T(256)S(1)}, f32[256]{0:T(256)}, u32[]{:S(2)}) copy-start(f32[256]{0:T(256)} %get-tuple-element.40) | copy-start | bytes 3076
  555.9 19.4 %copy-start.18 = (f32[256,256]{1,0:T(8,128)S(1)}, f32[256,256]{1,0:T(8,128)}, u32[]{:S(2)}) copy-start(f32[256,256]{1,0:T(8,128)} %fusion.141) | copy-start | bytes 786436
  581.9 5.8 collective-permute-start.2
  (20 other events, 70.3 us)
Sparse Core Ops, SparseCore 0:
  11.4 229.9 all-gather.2
  391.3 70.8 all-reduce.1
